TPU v7x, 32 devices: a whole 2x2x4 slice. The times are simulated.
32 devices in a mesh: seq: 8 (over z, x), rows: 4 (over y, core).
Axes of the slice: x: 2, y: 2, z: 4, core: 2. Of those that a mesh axis runs over, the one named last changes fastest.
Arguments:
- attn_in: bfloat16 [8192, 8192], P(('seq', 'rows')), may hold values from -6 to 6
- attn_out: bfloat16 [8192, 8192], P(('seq', 'rows')), may hold values from -6 to 6
- valid: int32 [8192], P(('seq', 'rows')), may hold values 0 or 1
- w_qkv: bfloat16 [10240, 8192], P('rows', 'seq'), may hold values from -6 to 6
- w_out: bfloat16 [8192, 8192], P('rows', 'seq'), may hold values from -6 to 6
- qkv_ranks: int32 [10240], P('rows'), may hold values from 3072 to 5120
- out_ranks: int32 [8192], P('rows'), may hold values from 3072 to 5120
Outputs:
- qkv_margins: float32 [10240, 8192], P('rows', 'seq')
- out_margins: float32 [8192, 8192], P('rows', 'seq')
Inputs may be any that keep to these rules, and one draw needn't show every extreme that they name: `qkv_ranks`: each row keeps between three and five eighths of its 8192 weights. `out_ranks`: each row keeps between three and five eighths of its 8192 weights.
All inputs are finite; a program needn't handle non-finite values. No bound on the sum of `valid` on one device may be relied on, other than what follows from the above.
Results may differ from a plain program's by a relative error of at most 0.0003.
Values may be sent and summed in bfloat16 or wider, within the bound.
A program may use at most 128 MiB of HBM per device.

v0:
```python
import jax
import jax.numpy as jnp
from jax import lax
from jax.sharding import PartitionSpec as P

EPS = 1e-06


def tile_scores(weights, norm):
    return jnp.abs(weights.astype(jnp.float32)) * norm[None, :]


def row_limits(scores, ranks):
    lower = jnp.zeros((scores.shape[0],), jnp.float32)
    upper = jnp.max(scores, axis=1) + 1.0

    def bisect(step, state):
        low, high = state
        middle = 0.5 * (low + high)
        counted = jnp.sum((scores >= middle[:, None]).astype(jnp.int32), axis=1)
        rising = counted >= ranks
        return (jnp.where(rising, middle, low), jnp.where(rising, high, middle))

    lower, upper = lax.fori_loop(0, 24, bisect, (lower, upper))
    start = jnp.min(jnp.where(scores >= lower[:, None], scores, jnp.inf), axis=1)

    def strictly_above(candidate):
        return jnp.sum((scores > candidate[:, None]).astype(jnp.int32), axis=1)

    def unfinished(candidate):
        return jnp.any(strictly_above(candidate) >= ranks)

    def advance(candidate):
        further = strictly_above(candidate) >= ranks
        following = jnp.min(jnp.where(scores > candidate[:, None], scores, jnp.inf), axis=1)
        return jnp.where(further, following, candidate)

    return lax.while_loop(unfinished, advance, start)


def clipped(scores, limits):
    return jnp.maximum(scores - limits[:, None], 0.0)


def per_device(attn_in, attn_out, valid, w_qkv, w_out, qkv_ranks, out_ranks):
    weight = valid.astype(jnp.float32)[:, None]

    def squares(acts):
        acts32 = acts.astype(jnp.float32)
        return jnp.sum(acts32 * acts32 * weight, axis=0)

    partial_sums = jnp.stack([squares(attn_in), squares(attn_out)])
    total_tokens = attn_in.shape[0] * lax.axis_size("seq") * lax.axis_size("rows")
    seq_index = lax.axis_index("seq")
    totals = lax.psum(partial_sums, ("seq", "rows"))
    full_norm = jnp.sqrt(totals / total_tokens + EPS)
    qkv_whole, out_whole = (
        lax.all_to_all(w_qkv, "seq", split_axis=0, concat_axis=1, tiled=True),
        lax.all_to_all(w_out, "seq", split_axis=0, concat_axis=1, tiled=True),
    )
    qkv_rows = tile_scores(qkv_whole, full_norm[0])
    out_rows = tile_scores(out_whole, full_norm[1])
    qkv_count = qkv_rows.shape[0]
    out_count = out_rows.shape[0]
    qkv_mine = lax.dynamic_slice_in_dim(qkv_ranks, seq_index * qkv_count, qkv_count)
    out_mine = lax.dynamic_slice_in_dim(out_ranks, seq_index * out_count, out_count)
    qkv_limits = row_limits(qkv_rows, qkv_mine)
    out_limits = row_limits(out_rows, out_mine)
    qkv_result, out_result = (
        lax.all_to_all(
            clipped(qkv_rows, qkv_limits), "seq", split_axis=1, concat_axis=0, tiled=True
        ),
        lax.all_to_all(
            clipped(out_rows, out_limits), "seq", split_axis=1, concat_axis=0, tiled=True
        ),
    )
    return (qkv_result, out_result)


def solution(mesh):
    placed = (
        P(("seq", "rows"), None),
        P(("seq", "rows"), None),
        P(("seq", "rows")),
        P("rows", "seq"),
        P("rows", "seq"),
        P("rows"),
        P("rows"),
    )
    return jax.shard_map(
        per_device,
        mesh=mesh,
        in_specs=placed,
        out_specs=(P("rows", "seq"), P("rows", "seq")),
        check_vma=False,
    )
```

profile of v0, /device:TPU:0, one launch (start us, length us, event | category | flops | bytes accessed | tf_op | source)
XLA Modules:
  0.0 824.9 jit_solution(17134786051954232279)
XLA Ops:
  7.2 7.3 all-to-all-start.2
  14.5 4.7 multiply_reduce_fusion.1
  22.7 165.7 %all-reduce.2.cloned.1.call-done = f32[2,8192]{1,0:T(2,128)} async-done(((f32[2,8192]{1,0:T(2,128)}), f32[2,8192]{1,0:T(2,128)}) %all-reduce.2.cloned.1.call-update) | async-done | bytes 65552 | tf_op jit(solution)/shard_map/psum | solution.py:55
  189.5 5.4 all-to-all-start
  204.4 122.3 %while.43 = (s32[]{:T(128)}, f32[256]{0:T(256)S(1)}, f32[256]{0:T(256)S(1)}, f32[256,8192]{1,0:T(8,128)}, s32[256]{0:T(256)}, /*index=5*/s32[]{:T(128)}, s32[]{:T(128)}) while((s32[]{:T(128)}, f32[256]{0:T(256)S(1)}, f32[256]{0:T(256)S(1)}, f32[256,8192]{1,0:T(8,128)}, s32[256]{0:T(256)}, /*index=5*/s32[]{:T(128)}, ...), condition=%wide.region_17.18_spmd.clone, body=%wide.region_15.17_spmd.clone.sunk | while | flops 6292995 | bytes 8402528 | solution.py:24
  209.5 4.4 convert_reduce_fusion.7
  214.6 4.4 convert_reduce_fusion.7
  326.7 4.5 fusion.10
  331.2 6.6 while.39
  337.8 7.1 fusion.11
  344.9 21.1 %all-to-all-start.3 = ((f32[256,8,1024]{2,0,1:T(8,128)}), f32[256,8,1024]{2,0,1:T(8,128)}, u32[]{:S(2)}, u32[]{:S(2)}) async-start(f32[256,8,1024]{2,0,1:T(8,128)} %fusion.11), calls=%async_computation.3 | async-start | bytes 16777216 | tf_op jit(solution)/shard_map/all_to_all | solution.py:73
  370.2 5.2 copy.11
  375.4 9.7 %broadcast_multiply_fusion = f32[320,8192]{1,0:T(8,128)} fusion(f32[320,8192]{1,0:T(8,128)} %bitcast.30, f32[8192]{0:T(1024)S(1)} %bitcast.34), kind=kLoop, calls=%fused_computation.39 | loop fusion | flops 2621440 | bytes 21004288 | tf_op jit(solution)/shard_map/mul | solution.py:10
  385.0 141.9 %while.42 = (s32[]{:T(128)}, f32[320]{0:T(512)S(1)}, f32[320]{0:T(512)S(1)}, f32[320,8192]{1,0:T(8,128)}, s32[320]{0:T(512)}, /*index=5*/s32[]{:T(128)}, s32[]{:T(128)}) while((s32[]{:T(128)}, f32[320]{0:T(512)S(1)}, f32[320]{0:T(512)S(1)}, f32[320,8192]{1,0:T(8,128)}, s32[320]{0:T(512)}, /*index=5*/s32[]{:T(128)}, s32[]{:T(128)}) %tuple.71), condition=%wide.region_6.7_spmd.clone, body=%wide.region_4.6_spmd.clone.sunk | while | flops 7866243 | bytes 10503136 | solution.py:24
  385.0 5.2 convert_reduce_fusion.6
  391.0 5.2 convert_reduce_fusion.6
  396.9 5.2 convert_reduce_fusion.6
  402.8 5.2 convert_reduce_fusion.6
  408.7 5.2 convert_reduce_fusion.6
  414.6 5.2 convert_reduce_fusion.6
  420.5 5.2 convert_reduce_fusion.6
  426.4 5.2 convert_reduce_fusion.6
  432.4 5.2 convert_reduce_fusion.6
  438.3 5.2 convert_reduce_fusion.6
  444.2 5.2 convert_reduce_fusion.6
  450.1 5.2 convert_reduce_fusion.6
  456.0 5.2 convert_reduce_fusion.6
  461.9 5.2 convert_reduce_fusion.6
  467.8 5.2 convert_reduce_fusion.6
  473.7 5.2 convert_reduce_fusion.6
  479.7 5.2 convert_reduce_fusion.6
  485.6 5.2 convert_reduce_fusion.6
  491.5 5.2 convert_reduce_fusion.6
  497.4 5.2 convert_reduce_fusion.6
  503.3 5.2 convert_reduce_fusion.6
  509.2 5.2 convert_reduce_fusion.6
  515.1 5.2 convert_reduce_fusion.6
  521.0 5.2 convert_reduce_fusion.6
  526.9 5.3 fusion.5
  532.2 24.8 %while.37 = (f32[320]{0:T(512)}, f32[320,8192]{1,0:T(8,128)}, s32[320]{0:T(512)}) while((f32[320]{0:T(512)}, f32[320,8192]{1,0:T(8,128)}, s32[320]{0:T(512)}) %tuple.87), condition=%region_11.14_spmd, body=%region_8.11_spmd | while | flops 23593280 | bytes 73417016 | solution.py:38
  532.2 5.2 convert_reduce_fusion
  539.6 5.3 fusion.1
  549.8 5.2 convert_reduce_fusion
  557.0 8.4 %fusion.6 = f32[320,8,1024]{2,0,1:T(8,128)} fusion(bf16[8,320,1024]{2,1,0:T(8,128)(2,1)} %all-to-all-done, f32[320]{0:T(512)} %get-tuple-element.95, f32[8,1024]{1,0:T(8,128)S(1)} %mul.81), kind=kLoop, calls=%fused_computation.25 | loop fusion | flops 13107200 | bytes 15762688 | tf_op jit(solution)/shard_map/max | solution.py:42
  565.4 5.1 all-to-all-start.1
  570.6 228.8 %all-to-all-done.1 = f32[320,8,1024]{2,0,1:T(8,128)} async-done(((f32[320,8,1024]{2,0,1:T(8,128)}), f32[320,8,1024]{2,0,1:T(8,128)}, u32[]{:S(2)}, u32[]{:S(2)}) %all-to-all-start.1) | async-done | bytes 10485792 | tf_op jit(solution)/shard_map/all_to_all | solution.py:70
  799.4 10.3 %copy.40 = f32[2560,1024]{1,0:T(8,128)} copy(f32[2560,1024]{1,0:T(8,128)} %bitcast.7) | data formatting | bytes 20971520
  809.6 8.4 %copy.41 = f32[2048,1024]{1,0:T(8,128)} copy(f32[2048,1024]{1,0:T(8,128)} %bitcast.13) | data formatting | bytes 16777216
  (197 shorter events, 161.7 us)
Async XLA Ops:
  7.2 7.4 copy-start.2
  7.2 182.3 %all-to-all-start.2 = ((bf16[8,256,1024]{2,1,0:T(8,128)(2,1)}), bf16[8,256,1024]{2,1,0:T(8,128)(2,1)}, u32[]{:S(2)}, u32[]{:S(2)}) async-start(bf16[8,256,1024]{2,1,0:T(8,128)(2,1)} %bitcast.33), calls=%async_computation.2 | async-start | bytes 8388608 | tf_op jit(solution)/shard_map/all_to_all | solution.py:59
  14.5 173.9 %all-reduce.2.cloned.1.call-start = ((), (), s32[]{:S(2)}) async-start(), calls=%async_computation.4 | async-start | bytes 131072 | tf_op jit(solution)/shard_map/psum | solution.py:55
  189.5 155.4 %all-to-all-start = ((bf16[8,320,1024]{2,1,0:T(8,128)(2,1)}), bf16[8,320,1024]{2,1,0:T(8,128)(2,1)}, u32[]{:S(2)}, u32[]{:S(2)}) async-start(bf16[8,320,1024]{2,1,0:T(8,128)(2,1)} %bitcast.32), calls=%async_computation | async-start | bytes 10485760 | tf_op jit(solution)/shard_map/all_to_all | solution.py:58
  344.9 220.5 %all-to-all-start.3 = ((f32[256,8,1024]{2,0,1:T(8,128)}), f32[256,8,1024]{2,0,1:T(8,128)}, u32[]{:S(2)}, u32[]{:S(2)}) async-start(f32[256,8,1024]{2,0,1:T(8,128)} %fusion.11), calls=%async_computation.3 | async-start | bytes 16777216 | tf_op jit(solution)/shard_map/all_to_all | solution.py:73
  539.6 7.0 copy-start
  565.4 233.9 %all-to-all-start.1 = ((f32[320,8,1024]{2,0,1:T(8,128)}), f32[320,8,1024]{2,0,1:T(8,128)}, u32[]{:S(2)}, u32[]{:S(2)}) async-start(f32[320,8,1024]{2,0,1:T(8,128)} %fusion.6), calls=%async_computation.1 | async-start | bytes 20971520 | tf_op jit(solution)/shard_map/all_to_all | solution.py:70
Sparse Core Ops, SparseCore 0:
  21.4 166.8 all-reduce.1
where the time goes:
time: 829 us; the launch traced here: 825 us
  waiting for transfers between devices  394 us (48%)
  other arithmetic  344 us (41%)
  starting transfers between devices  39 us (5%)
  local copies, waits for them, and re-layouts  30.1 us (4%)
  between operations  14.2 us (2%)
    reduce_sum x48, other arithmetic, bisect(): counted = jnp.sum((scores >= middle[:, None]).astype(jnp.int32), axis=1)  229 us
    all_to_all x1, waiting for transfers between devices, per_device(): lax.all_to_all(clipped(qkv_rows, qkv_limits), 'seq', split_axis=1, concat...  229 us
    psum x1, waiting for transfers between devices, per_device(): totals = lax.psum(partial_sums, ('seq', 'rows'))  166 us
    select_n x96, other arithmetic, bisect(): return (jnp.where(rising, middle, low), jnp.where(rising, high, middle))  33.9 us
    all_to_all x1, starting transfers between devices, per_device(): lax.all_to_all(clipped(out_rows, out_limits), 'seq', split_axis=1, concat...  21.1 us
    unnamed x4, local copies, waits for them, and re-layouts  18.7 us
    reduce_sum x4, other arithmetic, strictly_above(): return jnp.sum((scores > candidate[:, None]).astype(jnp.int32), axis=1)  16.6 us
  transfers between devices with their start and end apart: 5, of which 2 were waited for; matrix products, arithmetic and copies ran while one was open for 43% of the time, Pallas kernels for 0%

commit v1 on v0

--- a/solution.py
+++ b/solution.py
@@ -67,8 +67,14 @@
     qkv_limits = row_limits(qkv_rows, qkv_mine)
     out_limits = row_limits(out_rows, out_mine)
     qkv_result, out_result = (
-        lax.all_to_all(
-            clipped(qkv_rows, qkv_limits), "seq", split_axis=1, concat_axis=0, tiled=True
+        jnp.concatenate(
+            lax.all_to_all(
+                jnp.stack(jnp.split(clipped(qkv_rows, qkv_limits), lax.axis_size("seq"), axis=1)),
+                "seq",
+                0,
+                0,
+            ),
+            axis=0,
         ),
         lax.all_to_all(
             clipped(out_rows, out_limits), "seq", split_axis=1, concat_axis=0, tiled=True

time: 829 us -> 847 us (1.022)
  local copies, waits for them, and re-layouts: 30.1 us -> 51.6 us
    unnamed x4 -> x15, local copies, waits for them, and re-layouts: 18.7 us -> 37.8 us
  transfers between devices with their start and end apart: 5 -> 5, of which waited for: 2 -> 2; matrix products, arithmetic and copies ran while one was open for 43% -> 44% of each run, Pallas kernels for 0% -> 0%
where the time goes in v1:
time: 847 us; the launch traced here: 843 us
  waiting for transfers between devices  395 us (47%)
  other arithmetic  341 us (40%)
  local copies, waits for them, and re-layouts  51.6 us (6%)
  starting transfers between devices  38.9 us (5%)
  between operations  14.2 us (2%)
    reduce_sum x48, other arithmetic, bisect(): counted = jnp.sum((scores >= middle[:, None]).astype(jnp.int32), axis=1)  229 us
    all_to_all x1, waiting for transfers between devices, per_device(): lax.all_to_all(jnp.stack(jnp.split(clipped(qkv_rows, qkv_limits), lax.axi...  229 us
    psum x1, waiting for transfers between devices, per_device(): totals = lax.psum(partial_sums, ('seq', 'rows'))  166 us
    unnamed x15, local copies, waits for them, and re-layouts  37.8 us
    select_n x96, other arithmetic, bisect(): return (jnp.where(rising, middle, low), jnp.where(rising, high, middle))  32.6 us
    all_to_all x1, starting transfers between devices, per_device(): lax.all_to_all(clipped(out_rows, out_limits), 'seq', split_axis=1, concat...  21 us
    reduce_sum x4, other arithmetic, strictly_above(): return jnp.sum((scores > candidate[:, None]).astype(jnp.int32), axis=1)  20.2 us
  transfers between devices with their start and end apart: 5, of which 2 were waited for; matrix products, arithmetic and copies ran while one was open for 44% of the time, Pallas kernels for 0%

profile of v1, /device:TPU:0, one launch (start us, length us, event | category | flops | bytes accessed | tf_op | source)
XLA Modules:
  0.0 843.4 jit_solution(9285544346414421268)
XLA Ops:
  7.2 7.3 all-to-all-start.2
  14.5 4.7 multiply_reduce_fusion.1
  22.6 165.7 %all-reduce.2.cloned.1.call-done = f32[2,8192]{1,0:T(2,128)} async-done(((f32[2,8192]{1,0:T(2,128)}), f32[2,8192]{1,0:T(2,128)}) %all-reduce.2.cloned.1.call-update) | async-done | bytes 65552 | tf_op jit(solution)/shard_map/psum | solution.py:55
  189.6 5.4 all-to-all-start
  204.4 122.3 %while.43 = (s32[]{:T(128)}, f32[256]{0:T(256)S(1)}, f32[256]{0:T(256)S(1)}, f32[256,8192]{1,0:T(8,128)}, s32[256]{0:T(256)}, /*index=5*/s32[]{:T(128)}, s32[]{:T(128)}) while((s32[]{:T(128)}, f32[256]{0:T(256)S(1)}, f32[256]{0:T(256)S(1)}, f32[256,8192]{1,0:T(8,128)}, s32[256]{0:T(256)}, /*index=5*/s32[]{:T(128)}, ...), condition=%wide.region_17.18_spmd.clone, body=%wide.region_15.17_spmd.clone.sunk | while | flops 6292995 | bytes 8402520 | solution.py:24
  209.5 4.4 convert_reduce_fusion.7
  326.7 4.5 fusion.9
  331.2 6.5 while.39
  337.7 7.1 fusion.10
  344.9 21.0 %all-to-all-start.3 = ((f32[256,8,1024]{2,0,1:T(8,128)}), f32[256,8,1024]{2,0,1:T(8,128)}, u32[]{:S(2)}, u32[]{:S(2)}) async-start(f32[256,8,1024]{2,0,1:T(8,128)} %fusion.10), calls=%async_computation.3 | async-start | bytes 16777216 | tf_op jit(solution)/shard_map/all_to_all | solution.py:79
  365.9 8.0 fusion.8
  373.9 5.1 copy.14
  379.0 5.7 broadcast_multiply_fusion
  386.0 140.6 %while.42 = (s32[]{:T(128)}, f32[320]{0:T(512)S(1)}, f32[320]{0:T(512)S(1)}, f32[320,8192]{1,0:T(8,128)}, s32[320]{0:T(512)}, /*index=5*/s32[]{:T(128)}, s32[]{:T(128)}) while((s32[]{:T(128)}, f32[320]{0:T(512)S(1)}, f32[320]{0:T(512)S(1)}, f32[320,8192]{1,0:T(8,128)}, s32[320]{0:T(512)}, /*index=5*/s32[]{:T(128)}, s32[]{:T(128)}) %tuple.71), condition=%wide.region_6.7_spmd.clone, body=%wide.region_4.6_spmd.clone.sunk | while | flops 7866243 | bytes 10503128 | solution.py:24
  386.0 5.2 convert_reduce_fusion.6
  391.9 5.2 convert_reduce_fusion.6
  397.8 5.2 convert_reduce_fusion.6
  403.6 5.2 convert_reduce_fusion.6
  409.5 5.2 convert_reduce_fusion.6
  415.3 5.2 convert_reduce_fusion.6
  421.2 5.2 convert_reduce_fusion.6
  427.1 5.2 convert_reduce_fusion.6
  432.9 5.2 convert_reduce_fusion.6
  438.8 5.2 convert_reduce_fusion.6
  444.6 5.2 convert_reduce_fusion.6
  450.5 5.2 convert_reduce_fusion.6
  456.4 5.2 convert_reduce_fusion.6
  462.2 5.2 convert_reduce_fusion.6
  468.1 5.2 convert_reduce_fusion.6
  473.9 5.2 convert_reduce_fusion.6
  479.8 5.2 convert_reduce_fusion.6
  485.6 5.2 convert_reduce_fusion.6
  491.5 5.2 convert_reduce_fusion.6
  497.4 5.2 convert_reduce_fusion.6
  503.2 5.2 convert_reduce_fusion.6
  509.1 5.2 convert_reduce_fusion.6
  514.9 5.2 convert_reduce_fusion.6
  520.8 5.2 convert_reduce_fusion.6
  526.6 5.3 fusion.5
  531.9 25.1 %while.37 = (f32[320]{0:T(512)}, f32[320,8192]{1,0:T(8,128)}, s32[320]{0:T(512)}) while((f32[320]{0:T(512)}, f32[320,8192]{1,0:T(8,128)}, s32[320]{0:T(512)}) %tuple.87), condition=%region_11.14_spmd, body=%region_8.11_spmd | while | flops 23593280 | bytes 73417016 | solution.py:38
  531.9 5.3 convert_reduce_fusion
  539.9 5.3 fusion
  550.0 5.2 convert_reduce_fusion
  557.0 6.6 subtract_maximum_fusion
  583.9 5.1 all-to-all-start.1
  589.0 228.8 %all-to-all-done.1 = f32[8,320,1024]{2,1,0:T(8,128)} async-done(((f32[8,320,1024]{2,1,0:T(8,128)}), f32[8,320,1024]{2,1,0:T(8,128)}, u32[]{:S(2)}, u32[]{:S(2)}) %all-to-all-start.1) | async-done | bytes 10485792 | tf_op jit(solution)/shard_map/all_to_all | solution.py:71
  817.8 10.3 %copy.50 = f32[2560,1024]{1,0:T(8,128)} copy(f32[2560,1024]{1,0:T(8,128)} %bitcast.14) | data formatting | bytes 20971520
  828.1 8.4 %copy.51 = f32[2048,1024]{1,0:T(8,128)} copy(f32[2048,1024]{1,0:T(8,128)} %bitcast.20) | data formatting | bytes 16777216
  (209 shorter events, 182.6 us)
Async XLA Ops:
  7.2 7.4 copy-start.4
  7.2 182.4 %all-to-all-start.2 = ((bf16[8,256,1024]{2,1,0:T(8,128)(2,1)}), bf16[8,256,1024]{2,1,0:T(8,128)(2,1)}, u32[]{:S(2)}, u32[]{:S(2)}) async-start(bf16[8,256,1024]{2,1,0:T(8,128)(2,1)} %bitcast.61), calls=%async_computation.2 | async-start | bytes 8388608 | tf_op jit(solution)/shard_map/all_to_all | solution.py:59
  14.5 173.9 %all-reduce.2.cloned.1.call-start = ((), (), s32[]{:S(2)}) async-start(), calls=%async_computation.4 | async-start | bytes 131072 | tf_op jit(solution)/shard_map/psum | solution.py:55
  189.6 155.3 %all-to-all-start = ((bf16[8,320,1024]{2,1,0:T(8,128)(2,1)}), bf16[8,320,1024]{2,1,0:T(8,128)(2,1)}, u32[]{:S(2)}, u32[]{:S(2)}) async-start(bf16[8,320,1024]{2,1,0:T(8,128)(2,1)} %bitcast.60), calls=%async_computation | async-start | bytes 10485760 | tf_op jit(solution)/shard_map/all_to_all | solution.py:58
  344.9 239.0 %all-to-all-start.3 = ((f32[256,8,1024]{2,0,1:T(8,128)}), f32[256,8,1024]{2,0,1:T(8,128)}, u32[]{:S(2)}, u32[]{:S(2)}) async-start(f32[256,8,1024]{2,0,1:T(8,128)} %fusion.10), calls=%async_computation.3 | async-start | bytes 16777216 | tf_op jit(solution)/shard_map/all_to_all | solution.py:79
  379.0 7.0 copy-start.2
  531.9 25.1 %copy-start.3 = (f32[8,40,8,1024]{3,2,0,1:T(8,128)S(1)}, f32[8,40,8,1024]{3,2,0,1:T(8,128)}, u32[]{:S(2)}) copy-start(f32[8,40,8,1024]{3,2,0,1:T(8,128)} %copy-done.2) | copy-start | bytes 31457284
  539.9 7.0 copy-start
  583.9 234.0 %all-to-all-start.1 = ((f32[8,320,1024]{2,1,0:T(8,128)}), f32[8,320,1024]{2,1,0:T(8,128)}, u32[]{:S(2)}, u32[]{:S(2)}) async-start(f32[8,320,1024]{2,1,0:T(8,128)} %fusion.14), calls=%async_computation.1 | async-start | bytes 20971520 | tf_op jit(solution)/shard_map/all_to_all | solution.py:71
Sparse Core Ops, SparseCore 0:
  21.4 166.9 all-reduce.1
